TPU v7x, 32 devices: a 4x4x1 block of a 4x4x8 slice. The times are simulated.
32 devices in a mesh: dp: 1 (over z), sp: 32 (over y, x, core).
Axes of the slice: x: 4, y: 4, z: 1, core: 2. Of those that a mesh axis runs over, the one named last changes fastest.
The devices are a block of a 4x4x8 slice.
Arguments:
- x: bfloat16 [16, 1024, 256], P('dp', 'sp')
- w_cur: bfloat16 [16, 8, 256, 512], replicated
- w_past: bfloat16 [16, 8, 256, 512], replicated
- w_res: bfloat16 [16, 8, 256, 256], replicated
- w_skip: bfloat16 [16, 8, 256, 256], replicated
Outputs:
- output 1: float32 [16, 32, 32, 256], P('dp', 'sp')
- output 2: float32 [16, 32, 32, 256], P('dp', 'sp')
All inputs are finite; a program needn't handle non-finite values.
Results may differ from a plain program's by a relative error of at most 0.0089469.
Values are sent between devices in bfloat16 or wider.
A program may use at most 768 MiB of HBM per device.

v0:
```python
import jax
import jax.numpy as jnp
from jax import lax
from jax.sharding import PartitionSpec as P


def solution(mesh):
    group_n = mesh.shape["sp"]

    def past_rows(u_cur, dilation):
        seq_dev = u_cur.shape[1]
        if dilation < seq_dev:
            halo_rows = lax.ppermute(u_cur[:, seq_dev - dilation:], "sp", [(source, source + 1) for source in range(group_n - 1)])
            return jnp.concatenate([halo_rows, u_cur[:, :seq_dev - dilation]], axis=1)
        hop_count = dilation // seq_dev
        return lax.ppermute(u_cur, "sp", [(source, source + hop_count) for source in range(group_n - hop_count)])

    def to_cyclic(local_rows):
        batch_n, seq_dev, feat_width = local_rows.shape
        grid_rows = local_rows.reshape(batch_n, seq_dev // group_n, group_n, feat_width)
        received = lax.all_to_all(grid_rows, "sp", 2, 1, tiled=True)
        return received.reshape(batch_n, 1, seq_dev, feat_width)

    def local_stack(x_loc, w_cur, w_past, w_res, w_skip):
        channels = x_loc.shape[-1]
        stacks, cycle_len = w_cur.shape[0], w_cur.shape[1]
        h_res = x_loc.astype(jnp.float32)
        skip_acc = jnp.zeros((x_loc.shape[0], x_loc.shape[1], w_skip.shape[-1]), jnp.float32)
        for stack_pos in range(stacks):
            for layer_pos in range(cycle_len):
                u_cur = h_res.astype(jnp.bfloat16)
                u_past = past_rows(u_cur, 2 ** layer_pos)
                pre_act = jnp.einsum("bsc,cd->bsd", u_cur, w_cur[stack_pos, layer_pos], preferred_element_type=jnp.float32) + jnp.einsum("bsc,cd->bsd", u_past, w_past[stack_pos, layer_pos], preferred_element_type=jnp.float32)
                gated = (jnp.tanh(pre_act[..., :channels]) * jax.nn.sigmoid(pre_act[..., channels:])).astype(jnp.bfloat16)
                h_res = h_res + jnp.einsum("bsc,cd->bsd", gated, w_res[stack_pos, layer_pos], preferred_element_type=jnp.float32)
                skip_acc = skip_acc + jnp.einsum("bsc,cd->bsd", gated, w_skip[stack_pos, layer_pos], preferred_element_type=jnp.float32)
        return to_cyclic(h_res), to_cyclic(skip_acc)

    return jax.shard_map(local_stack, mesh=mesh, in_specs=(P("dp", "sp", None), P(), P(), P(), P()), out_specs=(P("dp", "sp", None, None), P("dp", "sp", None, None)), check_vma=False)
```

profile of v0, /device:TPU:97, one launch (start us, length us, event | category | flops | bytes accessed | tf_op | source)
XLA Modules:
  0.0 1574.5 jit_solution(3046084086787453864)
XLA Ops:
  68.1 14.1 collective-permute-start.7
  89.3 7.7 collective-permute-start.8
  162.7 16.1 %collective-permute-start.15 = (bf16[16,32,256]{2,1,0:T(8,128)(2,1)S(1)}, bf16[16,32,256]{2,1,0:T(8,128)(2,1)S(1)}, u32[]{:S(2)}, u32[]{:S(2)}) collective-permute-start(bf16[16,32,256]{2,1,0:T(8,128)(2,1)S(1)} %get-tuple-element.66), channel_id=1, source_target_pairs={{0,4},{1,5},{2,6},{3,7},{4,8},{5,9},{6,10},{7,11},{8,12},{9,13},{1... | collective-permute-start | bytes 786440 | tf_op jit(solution)/shard_map/ppermute | solution.py:16
  259.0 16.0 %collective-permute-start.23 = (bf16[16,32,256]{2,1,0:T(8,128)(2,1)S(1)}, bf16[16,32,256]{2,1,0:T(8,128)(2,1)S(1)}, u32[]{:S(2)}, u32[]{:S(2)}) collective-permute-start(bf16[16,32,256]{2,1,0:T(8,128)(2,1)S(1)} %get-tuple-element.82), channel_id=1, source_target_pairs={{0,4},{1,5},{2,6},{3,7},{4,8},{5,9},{6,10},{7,11},{8,12},{9,13},{1... | collective-permute-start | bytes 786440 | tf_op jit(solution)/shard_map/ppermute | solution.py:16
  282.2 7.8 collective-permute-start.24
  355.3 15.9 %collective-permute-start.31 = (bf16[16,32,256]{2,1,0:T(8,128)(2,1)S(1)}, bf16[16,32,256]{2,1,0:T(8,128)(2,1)S(1)}, u32[]{:S(2)}, u32[]{:S(2)}) collective-permute-start(bf16[16,32,256]{2,1,0:T(8,128)(2,1)S(1)} %get-tuple-element.98), channel_id=1, source_target_pairs={{0,4},{1,5},{2,6},{3,7},{4,8},{5,9},{6,10},{7,11},{8,12},{9,13},{1... | collective-permute-start | bytes 786440 | tf_op jit(solution)/shard_map/ppermute | solution.py:16
  378.3 7.7 collective-permute-start.32
  451.3 16.1 %collective-permute-start.39 = (bf16[16,32,256]{2,1,0:T(8,128)(2,1)S(1)}, bf16[16,32,256]{2,1,0:T(8,128)(2,1)S(1)}, u32[]{:S(2)}, u32[]{:S(2)}) collective-permute-start(bf16[16,32,256]{2,1,0:T(8,128)(2,1)S(1)} %get-tuple-element.114), channel_id=1, source_target_pairs={{0,4},{1,5},{2,6},{3,7},{4,8},{5,9},{6,10},{7,11},{8,12},{9,13},{1... | collective-permute-start | bytes 786440 | tf_op jit(solution)/shard_map/ppermute | solution.py:16
  474.5 7.7 collective-permute-start.40
  547.5 16.1 %collective-permute-start.47 = (bf16[16,32,256]{2,1,0:T(8,128)(2,1)S(1)}, bf16[16,32,256]{2,1,0:T(8,128)(2,1)S(1)}, u32[]{:S(2)}, u32[]{:S(2)}) collective-permute-start(bf16[16,32,256]{2,1,0:T(8,128)(2,1)S(1)} %get-tuple-element.130), channel_id=1, source_target_pairs={{0,4},{1,5},{2,6},{3,7},{4,8},{5,9},{6,10},{7,11},{8,12},{9,13},{1... | collective-permute-start | bytes 786440 | tf_op jit(solution)/shard_map/ppermute | solution.py:16
  570.7 8.1 collective-permute-start.48
  644.1 15.7 collective-permute-start.55
  666.9 7.7 collective-permute-start.56
  739.8 16.1 %collective-permute-start.63 = (bf16[16,32,256]{2,1,0:T(8,128)(2,1)S(1)}, bf16[16,32,256]{2,1,0:T(8,128)(2,1)S(1)}, u32[]{:S(2)}, u32[]{:S(2)}) collective-permute-start(bf16[16,32,256]{2,1,0:T(8,128)(2,1)S(1)} %get-tuple-element.162), channel_id=1, source_target_pairs={{0,4},{1,5},{2,6},{3,7},{4,8},{5,9},{6,10},{7,11},{8,12},{9,13},{1... | collective-permute-start | bytes 786440 | tf_op jit(solution)/shard_map/ppermute | solution.py:16
  763.1 7.7 collective-permute-start.64
  836.0 16.1 %collective-permute-start.71 = (bf16[16,32,256]{2,1,0:T(8,128)(2,1)S(1)}, bf16[16,32,256]{2,1,0:T(8,128)(2,1)S(1)}, u32[]{:S(2)}, u32[]{:S(2)}) collective-permute-start(bf16[16,32,256]{2,1,0:T(8,128)(2,1)S(1)} %get-tuple-element.178), channel_id=1, source_target_pairs={{0,4},{1,5},{2,6},{3,7},{4,8},{5,9},{6,10},{7,11},{8,12},{9,13},{1... | collective-permute-start | bytes 786440 | tf_op jit(solution)/shard_map/ppermute | solution.py:16
  859.3 7.9 collective-permute-start.72
  932.4 15.8 %collective-permute-start.79 = (bf16[16,32,256]{2,1,0:T(8,128)(2,1)S(1)}, bf16[16,32,256]{2,1,0:T(8,128)(2,1)S(1)}, u32[]{:S(2)}, u32[]{:S(2)}) collective-permute-start(bf16[16,32,256]{2,1,0:T(8,128)(2,1)S(1)} %get-tuple-element.194), channel_id=1, source_target_pairs={{0,4},{1,5},{2,6},{3,7},{4,8},{5,9},{6,10},{7,11},{8,12},{9,13},{1... | collective-permute-start | bytes 786440 | tf_op jit(solution)/shard_map/ppermute | solution.py:16
  955.5 7.7 collective-permute-start.80
  1028.4 16.1 %collective-permute-start.87 = (bf16[16,32,256]{2,1,0:T(8,128)(2,1)S(1)}, bf16[16,32,256]{2,1,0:T(8,128)(2,1)S(1)}, u32[]{:S(2)}, u32[]{:S(2)}) collective-permute-start(bf16[16,32,256]{2,1,0:T(8,128)(2,1)S(1)} %get-tuple-element.210), channel_id=1, source_target_pairs={{0,4},{1,5},{2,6},{3,7},{4,8},{5,9},{6,10},{7,11},{8,12},{9,13},{1... | collective-permute-start | bytes 786440 | tf_op jit(solution)/shard_map/ppermute | solution.py:16
  1051.6 7.7 collective-permute-start.88
  1124.6 16.1 %collective-permute-start.95 = (bf16[16,32,256]{2,1,0:T(8,128)(2,1)S(1)}, bf16[16,32,256]{2,1,0:T(8,128)(2,1)S(1)}, u32[]{:S(2)}, u32[]{:S(2)}) collective-permute-start(bf16[16,32,256]{2,1,0:T(8,128)(2,1)S(1)} %get-tuple-element.226), channel_id=1, source_target_pairs={{0,4},{1,5},{2,6},{3,7},{4,8},{5,9},{6,10},{7,11},{8,12},{9,13},{1... | collective-permute-start | bytes 786440 | tf_op jit(solution)/shard_map/ppermute | solution.py:16
  1147.8 7.8 collective-permute-start.96
  1221.0 15.9 %collective-permute-start.103 = (bf16[16,32,256]{2,1,0:T(8,128)(2,1)S(1)}, bf16[16,32,256]{2,1,0:T(8,128)(2,1)S(1)}, u32[]{:S(2)}, u32[]{:S(2)}) collective-permute-start(bf16[16,32,256]{2,1,0:T(8,128)(2,1)S(1)} %get-tuple-element.242), channel_id=1, source_target_pairs={{0,4},{1,5},{2,6},{3,7},{4,8},{5,9},{6,10},{7,11},{8,12},{9,13},{1... | collective-permute-start | bytes 786440 | tf_op jit(solution)/shard_map/ppermute | solution.py:16
  1244.0 7.7 collective-permute-start.104
  1317.0 16.1 %collective-permute-start.111 = (bf16[16,32,256]{2,1,0:T(8,128)(2,1)S(1)}, bf16[16,32,256]{2,1,0:T(8,128)(2,1)S(1)}, u32[]{:S(2)}, u32[]{:S(2)}) collective-permute-start(bf16[16,32,256]{2,1,0:T(8,128)(2,1)S(1)} %get-tuple-element.258), channel_id=1, source_target_pairs={{0,4},{1,5},{2,6},{3,7},{4,8},{5,9},{6,10},{7,11},{8,12},{9,13},{1... | collective-permute-start | bytes 786440 | tf_op jit(solution)/shard_map/ppermute | solution.py:16
  1413.1 16.1 %collective-permute-start.119 = (bf16[16,32,256]{2,1,0:T(8,128)(2,1)S(1)}, bf16[16,32,256]{2,1,0:T(8,128)(2,1)S(1)}, u32[]{:S(2)}, u32[]{:S(2)}) collective-permute-start(bf16[16,32,256]{2,1,0:T(8,128)(2,1)S(1)} %get-tuple-element.274), channel_id=1, source_target_pairs={{0,4},{1,5},{2,6},{3,7},{4,8},{5,9},{6,10},{7,11},{8,12},{9,13},{1... | collective-permute-start | bytes 786440 | tf_op jit(solution)/shard_map/ppermute | solution.py:16
  1436.4 7.9 collective-permute-start.120
  1509.6 15.8 %collective-permute-start.127 = (bf16[16,32,256]{2,1,0:T(8,128)(2,1)S(1)}, bf16[16,32,256]{2,1,0:T(8,128)(2,1)S(1)}, u32[]{:S(2)}, u32[]{:S(2)}) collective-permute-start(bf16[16,32,256]{2,1,0:T(8,128)(2,1)S(1)} %get-tuple-element.290), channel_id=1, source_target_pairs={{0,4},{1,5},{2,6},{3,7},{4,8},{5,9},{6,10},{7,11},{8,12},{9,13},{1... | collective-permute-start | bytes 786440 | tf_op jit(solution)/shard_map/ppermute | solution.py:16
  1532.4 14.9 all-to-all-start.1
  1549.6 8.8 all-to-all-done.1
  1563.1 9.9 all-to-all-done
  (968 shorter events, 1179.2 us)
Async XLA Ops:
  68.1 17.4 %collective-permute-start.7 = (bf16[16,32,256]{2,1,0:T(8,128)(2,1)S(1)}, bf16[16,32,256]{2,1,0:T(8,128)(2,1)S(1)}, u32[]{:S(2)}, u32[]{:S(2)}) collective-permute-start(bf16[16,32,256]{2,1,0:T(8,128)(2,1)S(1)} %get-tuple-element.50), channel_id=1, source_target_pairs={{0,4},{1,5},{2,6},{3,7},{4,8},{5,9},{6,10},{7,11},{8,12},{9,13},{1... | collective-permute-start | bytes 786440 | tf_op jit(solution)/shard_map/ppermute | solution.py:16
  149.0 11.1 collective-permute-start.14
  162.7 19.4 %collective-permute-start.15 = (bf16[16,32,256]{2,1,0:T(8,128)(2,1)S(1)}, bf16[16,32,256]{2,1,0:T(8,128)(2,1)S(1)}, u32[]{:S(2)}, u32[]{:S(2)}) collective-permute-start(bf16[16,32,256]{2,1,0:T(8,128)(2,1)S(1)} %get-tuple-element.66), channel_id=1, source_target_pairs={{0,4},{1,5},{2,6},{3,7},{4,8},{5,9},{6,10},{7,11},{8,12},{9,13},{1... | collective-permute-start | bytes 786440 | tf_op jit(solution)/shard_map/ppermute | solution.py:16
  245.2 11.1 collective-permute-start.22
  259.0 19.3 %collective-permute-start.23 = (bf16[16,32,256]{2,1,0:T(8,128)(2,1)S(1)}, bf16[16,32,256]{2,1,0:T(8,128)(2,1)S(1)}, u32[]{:S(2)}, u32[]{:S(2)}) collective-permute-start(bf16[16,32,256]{2,1,0:T(8,128)(2,1)S(1)} %get-tuple-element.82), channel_id=1, source_target_pairs={{0,4},{1,5},{2,6},{3,7},{4,8},{5,9},{6,10},{7,11},{8,12},{9,13},{1... | collective-permute-start | bytes 786440 | tf_op jit(solution)/shard_map/ppermute | solution.py:16
  341.6 11.1 collective-permute-start.30
  355.3 19.1 %collective-permute-start.31 = (bf16[16,32,256]{2,1,0:T(8,128)(2,1)S(1)}, bf16[16,32,256]{2,1,0:T(8,128)(2,1)S(1)}, u32[]{:S(2)}, u32[]{:S(2)}) collective-permute-start(bf16[16,32,256]{2,1,0:T(8,128)(2,1)S(1)} %get-tuple-element.98), channel_id=1, source_target_pairs={{0,4},{1,5},{2,6},{3,7},{4,8},{5,9},{6,10},{7,11},{8,12},{9,13},{1... | collective-permute-start | bytes 786440 | tf_op jit(solution)/shard_map/ppermute | solution.py:16
  437.6 11.1 collective-permute-start.38
  451.3 19.3 %collective-permute-start.39 = (bf16[16,32,256]{2,1,0:T(8,128)(2,1)S(1)}, bf16[16,32,256]{2,1,0:T(8,128)(2,1)S(1)}, u32[]{:S(2)}, u32[]{:S(2)}) collective-permute-start(bf16[16,32,256]{2,1,0:T(8,128)(2,1)S(1)} %get-tuple-element.114), channel_id=1, source_target_pairs={{0,4},{1,5},{2,6},{3,7},{4,8},{5,9},{6,10},{7,11},{8,12},{9,13},{1... | collective-permute-start | bytes 786440 | tf_op jit(solution)/shard_map/ppermute | solution.py:16
  547.5 19.3 %collective-permute-start.47 = (bf16[16,32,256]{2,1,0:T(8,128)(2,1)S(1)}, bf16[16,32,256]{2,1,0:T(8,128)(2,1)S(1)}, u32[]{:S(2)}, u32[]{:S(2)}) collective-permute-start(bf16[16,32,256]{2,1,0:T(8,128)(2,1)S(1)} %get-tuple-element.130), channel_id=1, source_target_pairs={{0,4},{1,5},{2,6},{3,7},{4,8},{5,9},{6,10},{7,11},{8,12},{9,13},{1... | collective-permute-start | bytes 786440 | tf_op jit(solution)/shard_map/ppermute | solution.py:16
  630.3 11.1 collective-permute-start.54
  644.1 18.9 %collective-permute-start.55 = (bf16[16,32,256]{2,1,0:T(8,128)(2,1)S(1)}, bf16[16,32,256]{2,1,0:T(8,128)(2,1)S(1)}, u32[]{:S(2)}, u32[]{:S(2)}) collective-permute-start(bf16[16,32,256]{2,1,0:T(8,128)(2,1)S(1)} %get-tuple-element.146), channel_id=1, source_target_pairs={{0,4},{1,5},{2,6},{3,7},{4,8},{5,9},{6,10},{7,11},{8,12},{9,13},{1... | collective-permute-start | bytes 786440 | tf_op jit(solution)/shard_map/ppermute | solution.py:16
  726.1 11.1 collective-permute-start.62
  739.8 19.3 %collective-permute-start.63 = (bf16[16,32,256]{2,1,0:T(8,128)(2,1)S(1)}, bf16[16,32,256]{2,1,0:T(8,128)(2,1)S(1)}, u32[]{:S(2)}, u32[]{:S(2)}) collective-permute-start(bf16[16,32,256]{2,1,0:T(8,128)(2,1)S(1)} %get-tuple-element.162), channel_id=1, source_target_pairs={{0,4},{1,5},{2,6},{3,7},{4,8},{5,9},{6,10},{7,11},{8,12},{9,13},{1... | collective-permute-start | bytes 786440 | tf_op jit(solution)/shard_map/ppermute | solution.py:16
  822.3 11.1 collective-permute-start.70
  836.0 19.3 %collective-permute-start.71 = (bf16[16,32,256]{2,1,0:T(8,128)(2,1)S(1)}, bf16[16,32,256]{2,1,0:T(8,128)(2,1)S(1)}, u32[]{:S(2)}, u32[]{:S(2)}) collective-permute-start(bf16[16,32,256]{2,1,0:T(8,128)(2,1)S(1)} %get-tuple-element.178), channel_id=1, source_target_pairs={{0,4},{1,5},{2,6},{3,7},{4,8},{5,9},{6,10},{7,11},{8,12},{9,13},{1... | collective-permute-start | bytes 786440 | tf_op jit(solution)/shard_map/ppermute | solution.py:16
  918.7 11.1 collective-permute-start.78
  932.4 19.1 %collective-permute-start.79 = (bf16[16,32,256]{2,1,0:T(8,128)(2,1)S(1)}, bf16[16,32,256]{2,1,0:T(8,128)(2,1)S(1)}, u32[]{:S(2)}, u32[]{:S(2)}) collective-permute-start(bf16[16,32,256]{2,1,0:T(8,128)(2,1)S(1)} %get-tuple-element.194), channel_id=1, source_target_pairs={{0,4},{1,5},{2,6},{3,7},{4,8},{5,9},{6,10},{7,11},{8,12},{9,13},{1... | collective-permute-start | bytes 786440 | tf_op jit(solution)/shard_map/ppermute | solution.py:16
  1014.7 11.1 collective-permute-start.86
  1028.4 19.3 %collective-permute-start.87 = (bf16[16,32,256]{2,1,0:T(8,128)(2,1)S(1)}, bf16[16,32,256]{2,1,0:T(8,128)(2,1)S(1)}, u32[]{:S(2)}, u32[]{:S(2)}) collective-permute-start(bf16[16,32,256]{2,1,0:T(8,128)(2,1)S(1)} %get-tuple-element.210), channel_id=1, source_target_pairs={{0,4},{1,5},{2,6},{3,7},{4,8},{5,9},{6,10},{7,11},{8,12},{9,13},{1... | collective-permute-start | bytes 786440 | tf_op jit(solution)/shard_map/ppermute | solution.py:16
  1110.9 11.1 collective-permute-start.94
  1124.6 19.3 %collective-permute-start.95 = (bf16[16,32,256]{2,1,0:T(8,128)(2,1)S(1)}, bf16[16,32,256]{2,1,0:T(8,128)(2,1)S(1)}, u32[]{:S(2)}, u32[]{:S(2)}) collective-permute-start(bf16[16,32,256]{2,1,0:T(8,128)(2,1)S(1)} %get-tuple-element.226), channel_id=1, source_target_pairs={{0,4},{1,5},{2,6},{3,7},{4,8},{5,9},{6,10},{7,11},{8,12},{9,13},{1... | collective-permute-start | bytes 786440 | tf_op jit(solution)/shard_map/ppermute | solution.py:16
  1207.3 11.1 collective-permute-start.102
  1221.0 19.1 %collective-permute-start.103 = (bf16[16,32,256]{2,1,0:T(8,128)(2,1)S(1)}, bf16[16,32,256]{2,1,0:T(8,128)(2,1)S(1)}, u32[]{:S(2)}, u32[]{:S(2)}) collective-permute-start(bf16[16,32,256]{2,1,0:T(8,128)(2,1)S(1)} %get-tuple-element.242), channel_id=1, source_target_pairs={{0,4},{1,5},{2,6},{3,7},{4,8},{5,9},{6,10},{7,11},{8,12},{9,13},{1... | collective-permute-start | bytes 786440 | tf_op jit(solution)/shard_map/ppermute | solution.py:16
  1303.2 11.1 collective-permute-start.110
  1317.0 19.3 %collective-permute-start.111 = (bf16[16,32,256]{2,1,0:T(8,128)(2,1)S(1)}, bf16[16,32,256]{2,1,0:T(8,128)(2,1)S(1)}, u32[]{:S(2)}, u32[]{:S(2)}) collective-permute-start(bf16[16,32,256]{2,1,0:T(8,128)(2,1)S(1)} %get-tuple-element.258), channel_id=1, source_target_pairs={{0,4},{1,5},{2,6},{3,7},{4,8},{5,9},{6,10},{7,11},{8,12},{9,13},{1... | collective-permute-start | bytes 786440 | tf_op jit(solution)/shard_map/ppermute | solution.py:16
  1399.4 11.1 collective-permute-start.118
  1413.1 19.3 %collective-permute-start.119 = (bf16[16,32,256]{2,1,0:T(8,128)(2,1)S(1)}, bf16[16,32,256]{2,1,0:T(8,128)(2,1)S(1)}, u32[]{:S(2)}, u32[]{:S(2)}) collective-permute-start(bf16[16,32,256]{2,1,0:T(8,128)(2,1)S(1)} %get-tuple-element.274), channel_id=1, source_target_pairs={{0,4},{1,5},{2,6},{3,7},{4,8},{5,9},{6,10},{7,11},{8,12},{9,13},{1... | collective-permute-start | bytes 786440 | tf_op jit(solution)/shard_map/ppermute | solution.py:16
  1495.9 11.1 collective-permute-start.126
  1509.6 19.1 %collective-permute-start.127 = (bf16[16,32,256]{2,1,0:T(8,128)(2,1)S(1)}, bf16[16,32,256]{2,1,0:T(8,128)(2,1)S(1)}, u32[]{:S(2)}, u32[]{:S(2)}) collective-permute-start(bf16[16,32,256]{2,1,0:T(8,128)(2,1)S(1)} %get-tuple-element.290), channel_id=1, source_target_pairs={{0,4},{1,5},{2,6},{3,7},{4,8},{5,9},{6,10},{7,11},{8,12},{9,13},{1... | collective-permute-start | bytes 786440 | tf_op jit(solution)/shard_map/ppermute | solution.py:16
  1532.4 26.0 %all-to-all-start.1 = ((f32[16,1,32,256]{3,0,1,2:T(8,128)}), f32[16,1,32,256]{3,0,1,2:T(8,128)S(1)}, u32[]{:S(2)}, u32[]{:S(2)}) async-start(f32[16,1,32,256]{3,0,1,2:T(8,128)} %copy.10), calls=%async_computation.1 | async-start | bytes 1048576 | tf_op jit(solution)/shard_map/all_to_all | solution.py:21
  1558.4 14.6 all-to-all-start
  (98 other events, 631.8 us)
where the time goes:
time: 1600 us; the launch traced here: 1570 us
  starting transfers between devices  812 us (51%)
  matrix products  609 us (38%)
  waiting for transfers between devices  112 us (7%)
  other arithmetic  27.7 us (2%)
    ppermute x48, starting transfers between devices, past_rows(): lax.ppermute(u_cur, 'sp', [(source, source + hop_count) for source in ran...  409 us
    ppermute x80, starting transfers between devices, past_rows(): lax.ppermute(u_cur[:, seq_dev - dilation:], 'sp', [(source, source + 1) f...  384 us
    dot_general x128, matrix products, local_stack(): jnp.einsum('bsc,cd->bsd', u_past, w_past[stack_pos, layer_pos], preferred...  160 us
    dot_general x128, matrix products, local_stack(): jnp.einsum('bsc,cd->bsd', u_cur, w_cur[stack_pos, layer_pos], preferred_e...  159 us
    dot_general x128, matrix products, local_stack(): jnp.einsum('bsc,cd->bsd', gated, w_res[stack_pos, layer_pos], preferred_e...  145 us
    dot_general x128, matrix products, local_stack(): jnp.einsum('bsc,cd->bsd', gated, w_skip[stack_pos, layer_pos], preferred_...  145 us
    ppermute x48, waiting for transfers between devices, past_rows(): lax.ppermute(u_cur, 'sp', [(source, source + hop_count) for source in ran...  78.7 us
  transfers between devices with their start and end apart: 130, of which 82 were waited for; matrix products, arithmetic and copies ran while one was open for 13% of the time, Pallas kernels for 0%

commit v1 on v0

v1 whole, which is shorter than its diff:
```python
import functools

import jax
import jax.numpy as jnp
from jax import lax
from jax.experimental import pallas as pl
from jax.experimental.pallas import tpu as pltpu
from jax.sharding import PartitionSpec as P

F32, BF16 = jnp.float32, jnp.bfloat16
LANES = 128


def load_rows(ref, start, count):
    return jnp.concatenate([ref[g, pl.ds(start, count), :] for g in range(ref.shape[0])], axis=1)


def store_rows(ref, start, value):
    for g in range(ref.shape[0]):
        ref[g, pl.ds(start, value.shape[0]), :] = value[:, g * LANES:(g + 1) * LANES]


def gated(z):
    c = z.shape[1] // 2
    return (jnp.tanh(z[:, :c]) * (0.5 * jnp.tanh(0.5 * z[:, c:]) + 0.5)).astype(BF16)


def stack_kernel(n, x_ref, wc, wp, wr, ws, out_ref, xbuf, h, skip, win, wout, halo_out, halo_in, stage,
                 w_sem, x_send, x_recv, halo_send, halo_recv, o_send, o_recv, self_sem):
    me = lax.axis_index("sp")
    batch, seq_dev = x_ref.shape[0], x_ref.shape[1]
    parts = n // batch
    srcs = n // parts
    rows = seq_dev * srcs
    stacks, cycle = wc.shape[0], wc.shape[1]
    reach = 2 ** (cycle - 1)
    seq, part = me // parts, lax.rem(me, parts)
    my_part = me // srcs

    def weight_copies(s, slot):
        return [pltpu.make_async_copy(w.at[s], buf.at[slot, t], w_sem.at[slot, 2 * o + t])
                for o, (buf, pair) in enumerate(((win, (wc, wp)), (wout, (wr, ws)))) for t, w in enumerate(pair)]

    for c in weight_copies(0, 0):
        c.start()
    halo_in[0] = jnp.zeros(halo_in.shape[1:], F32)
    skip[...] = jnp.zeros_like(skip)

    barrier = pltpu.get_barrier_semaphore()

    def greet(k, _):
        pl.semaphore_signal(barrier, inc=1, device_id={"sp": lax.rem(me + k, n)}, device_id_type=pl.DeviceIdType.MESH)
        return 0
    lax.fori_loop(1, n, greet, 0)
    pl.semaphore_wait(barrier, n - 1)

    slot_x = pl.ds(lax.rem(me, srcs) * seq_dev, seq_dev)

    def x_copy(b):
        return pltpu.make_async_remote_copy(
            src_ref=x_ref.at[b], dst_ref=xbuf.at[slot_x], send_sem=x_send.at[b], recv_sem=x_recv.at[lax.rem(me, srcs)],
            device_id={"sp": b * parts + my_part}, device_id_type=pl.DeviceIdType.MESH)

    def x_start(b, _):
        @pl.when(b * parts + my_part != me)
        def _():
            x_copy(b).start()

        @pl.when(b * parts + my_part == me)
        def _():
            pltpu.make_async_copy(x_ref.at[b], xbuf.at[slot_x], x_recv.at[lax.rem(me, srcs)]).start()
        return 0
    lax.fori_loop(0, batch, x_start, 0)

    def x_wait(i, _):
        pltpu.make_async_copy(x_ref.at[0], xbuf.at[pl.ds(i * seq_dev, seq_dev)], x_recv.at[i]).wait()
        return 0
    lax.fori_loop(0, srcs, x_wait, 0)
    store_rows(h.at[0], reach, xbuf[...].astype(F32))

    def layer(s, i, slot):
        src, dst = h.at[i % 2], h.at[(i + 1) % 2]
        d = 2 ** i
        for g in range(h.shape[1]):
            src[g, pl.ds(reach - d, d), :] = halo_in[s * part, g, pl.ds(d, d), :]
            halo_out[s, g, pl.ds(d, d), :] = src[g, pl.ds(reach + rows - d, d), :]
        cur = load_rows(src, reach, rows)
        past = load_rows(src, reach - d, rows).astype(BF16)
        z = (jnp.dot(cur.astype(BF16), win[slot, 0, i], preferred_element_type=F32)
             + jnp.dot(past, win[slot, 1, i], preferred_element_type=F32))
        a = gated(z)
        store_rows(dst, reach, cur + jnp.dot(a, wout[slot, 0, i], preferred_element_type=F32))
        store_rows(skip, 0, load_rows(skip, 0, rows) + jnp.dot(a, wout[slot, 1, i], preferred_element_type=F32))

    def halo_copy(s):
        return pltpu.make_async_remote_copy(
            src_ref=halo_out.at[s], dst_ref=halo_in.at[s], send_sem=halo_send.at[s], recv_sem=halo_recv.at[s],
            device_id={"sp": jnp.minimum(me + 1, n - 1)}, device_id_type=pl.DeviceIdType.MESH)

    def stack(s, _):
        slot = lax.rem(s, 2)
        for c in weight_copies(s, slot):
            c.wait()

        @pl.when(s + 1 < stacks)
        def _():
            for c in weight_copies(s + 1, 1 - slot):
                c.start()

        @pl.when(part > 0)
        def _():
            halo_copy(s).wait_recv()
        for i in range(cycle):
            layer(s, i, slot)

        @pl.when(part < parts - 1)
        def _():
            halo_copy(s).start()
        return 0
    lax.fori_loop(0, stacks, stack, 0)

    per = rows // n
    for j in range(n):
        for g in range(h.shape[1]):
            stage[j, 0, :, g * LANES:(g + 1) * LANES] = h[0, g, pl.ds(reach + j, per, stride=n), :]
            stage[j, 1, :, g * LANES:(g + 1) * LANES] = skip[g, pl.ds(j, per, stride=n), :]

    def out_copy(target, source):
        return pltpu.make_async_remote_copy(
            src_ref=stage.at[target], dst_ref=out_ref.at[source // parts, lax.rem(source, parts)],
            send_sem=o_send.at[target], recv_sem=o_recv.at[source],
            device_id={"sp": target}, device_id_type=pl.DeviceIdType.MESH)

    def out_start(k, _):
        out_copy(lax.rem(me + k, n), me).start()
        return 0
    lax.fori_loop(1, n, out_start, 0)
    own = pltpu.make_async_copy(stage.at[me], out_ref.at[seq, part], self_sem)
    own.start()

    def out_wait(k, _):
        other = lax.rem(me + k, n)
        out_copy(other, other).wait()
        return 0
    lax.fori_loop(1, n, out_wait, 0)
    own.wait()

    def x_done(b, _):
        @pl.when(b * parts + my_part != me)
        def _():
            x_copy(b).wait_send()
        return 0
    lax.fori_loop(0, batch, x_done, 0)

    @pl.when(part < parts - 1)
    def _():
        def sent(s, _):
            halo_copy(s).wait_send()
            return 0
        lax.fori_loop(0, stacks, sent, 0)


def solution(mesh):
    n = mesh.shape["sp"]

    def local_stack(x_loc, w_cur, w_past, w_res, w_skip):
        batch, seq_dev, channels = x_loc.shape
        stacks, cycle = w_cur.shape[:2]
        parts = n // batch
        srcs = n // parts
        rows, halves, reach = seq_dev * srcs, channels // LANES, 2 ** (cycle - 1)
        per = rows // n
        any_space = pl.BlockSpec(memory_space=pl.ANY)
        dma = pltpu.SemaphoreType.DMA
        out = pl.pallas_call(
            functools.partial(stack_kernel, n),
            out_shape=jax.ShapeDtypeStruct((batch, parts, 2, per, channels), F32),
            in_specs=[any_space] * 5,
            out_specs=any_space,
            scratch_shapes=[
                pltpu.VMEM((rows, channels), BF16),
                pltpu.VMEM((2, halves, reach + rows, LANES), F32),
                pltpu.VMEM((halves, rows, LANES), F32),
                pltpu.VMEM((2, 2) + w_cur.shape[1:], BF16),
                pltpu.VMEM((2, 2) + w_res.shape[1:], BF16),
                pltpu.VMEM((stacks, halves, 2 * reach, LANES), F32),
                pltpu.VMEM((stacks, halves, 2 * reach, LANES), F32),
                pltpu.VMEM((n, 2, per, channels), F32),
                dma((2, 4)), dma((batch,)), dma((srcs,)), dma((stacks,)), dma((stacks,)), dma((n,)), dma((n,)), dma,
            ],
            compiler_params=pltpu.CompilerParams(collective_id=0, has_side_effects=True, vmem_limit_bytes=56 << 20),
            name="conv_stack",
        )(x_loc, w_cur, w_past, w_res, w_skip)
        shape = (batch, 1, parts * per, channels)
        return out[:, :, 0].reshape(shape), out[:, :, 1].reshape(shape)

    return jax.shard_map(local_stack, mesh=mesh, in_specs=(P("dp", "sp", None), P(), P(), P(), P()), out_specs=(P("dp", "sp", None, None), P("dp", "sp", None, None)), check_vma=False)
```

time: 1600 us -> 93.3 us (0.06); the launches traced: 1570 us -> 93.2 us
  starting transfers between devices: 812 us -> 0 us
  matrix products: 609 us -> 0 us
  waiting for transfers between devices: 112 us -> 0 us
  Pallas kernels: 0 us -> 90.2 us
  other arithmetic: 27.7 us -> 0 us
    ppermute x128 -> x0, starting transfers between devices: 793 us -> none  [the longest x48 409 us: past_rows(): lax.ppermute(u_cur, 'sp', [(source, source + hop_count) for source in ran...]
    dot_general x512 -> x0, matrix products: 609 us -> none  [the longest x128 160 us: local_stack(): jnp.einsum('bsc,cd->bsd', u_past, w_past[stack_pos, layer_pos], preferred...]
    ppermute x128 -> x0, waiting for transfers between devices: 92.8 us -> none  [the longest x48 78.7 us: past_rows(): lax.ppermute(u_cur, 'sp', [(source, source + hop_count) for source in ran...]
    pallas_call x0 -> x1, Pallas kernels: none -> 90.2 us  [local_stack(): pl.pallas_call(functools.partial(stack_kernel, n), out_shape=jax.ShapeDty...]
    convert_element_type x128 -> x0, other arithmetic: 27.7 us -> none  [local_stack(): (jnp.tanh(pre_act[..., :channels]) * jax.nn.sigmoid(pre_act[..., channels...]
    all_to_all x2 -> x0, waiting for transfers between devices: 18.7 us -> none  [to_cyclic(): received = lax.all_to_all(grid_rows, 'sp', 2, 1, tiled=True)]
    all_to_all x2 -> x0, starting transfers between devices: 18.5 us -> none  [to_cyclic(): received = lax.all_to_all(grid_rows, 'sp', 2, 1, tiled=True)]
  transfers between devices with their start and end apart: 130 -> 0, of which waited for: 82 -> 0; matrix products, arithmetic and copies ran while one was open for 13% -> 0% of each run, Pallas kernels for 0% -> 0%
where the time goes in v1:
time: 93.3 us; the launch traced here: 93.2 us
  Pallas kernels  90.2 us (97%)
  local copies, waits for them, and re-layouts  2.29 us (2%)
    pallas_call x1, Pallas kernels, local_stack(): pl.pallas_call(functools.partial(stack_kernel, n), out_shape=jax.ShapeDty...  90.2 us
    slice x1, local copies, waits for them, and re-layouts, local_stack(): return (out[:, :, 0].reshape(shape), out[:, :, 1].reshape(shape))  2.29 us

profile of v1, /device:TPU:97, one launch (start us, length us, event | category | flops | bytes accessed | tf_op | source)
XLA Modules:
  0.0 93.2 jit_solution(12713391884184424387)
XLA Ops:
  0.6 90.2 %conv_stack.1 = f32[16,2,2,16,256]{4,3,2,1,0:T(8,128)} custom-call(bf16[16,32,256]{2,1,0:T(8,128)(2,1)} %x_ref.1, bf16[16,8,256,512]{3,2,1,0:T(8,128)(2,1)} %wc.1, bf16[16,8,256,512]{3,2,1,0:T(8,128)(2,1)} %wp.1, bf16[16,8,256,256]{3,2,1,0:T(8,128)(2,1)} %wr.1, bf16[16,8,256,256]{3,2,1,0:T(8,128)(2,1)} %ws.1), custom_call_target="tpu_custom_call" | custom-call | tf_op jit(solution)/shard_map/conv_stack/pallas_call | solution.py:175
  90.9 2.3 %fusion = (f32[16,2,1,16,256]{4,3,2,1,0:T(8,128)}, f32[16,2,1,16,256]{4,3,2,1,0:T(8,128)}) fusion(f32[16,2,2,16,256]{4,3,2,1,0:T(8,128)} %conv_stack.1), kind=kLoop, calls=%fused_computation | loop fusion | bytes 2097152 | tf_op jit(solution)/shard_map/slice | solution.py:195

commit v2 on v1

v2 whole, which is shorter than its diff:
```python
import functools
import math

import jax
import jax.numpy as jnp
from jax import lax
from jax.experimental import pallas as pl
from jax.experimental.pallas import tpu as pltpu
from jax.sharding import PartitionSpec as P

F32, BF16 = jnp.float32, jnp.bfloat16
LANES = 128
UNROLL = 2
VMEM = 50


def load_rows(ref, start, count):
    return jnp.concatenate([ref[g, pl.ds(start, count), :] for g in range(ref.shape[0])], axis=1)


def store_rows(ref, start, value):
    for g in range(ref.shape[0]):
        ref[g, pl.ds(start, value.shape[0]), :] = value[:, g * LANES:(g + 1) * LANES]


def gated(z):
    c = z.shape[1] // 2
    return (jnp.tanh(z[:, :c]) * (0.5 * jnp.tanh(0.5 * z[:, c:]) + 0.5)).astype(BF16)


def send_order(side, cores):
    def reach(v):
        return min(v, side - v)
    offsets = [(dx, dy, dc) for dc in range(cores) for dy in range(side) for dx in range(side)]
    return sorted(offsets, key=lambda o: -reach(o[0]) - reach(o[1]))


def stack_kernel(n, unroll, x_ref, wc, wp, wr, ws, out_ref, xv, xbuf, h, skip, win, wout, halo_out, halo_in, stage,
                 w_sem, x_send, x_recv, halo_send, halo_recv, o_send, o_recv, self_sem):
    me = lax.axis_index("sp")
    batch, seq_dev = x_ref.shape[0], x_ref.shape[1]
    parts = n // batch
    srcs = n // parts
    rows = seq_dev * srcs
    stacks, cycle = wc.shape[0], wc.shape[1]
    reach = 2 ** (cycle - 1)
    seq, part = me // parts, lax.rem(me, parts)
    my_part = me // srcs
    side = math.isqrt(batch)
    chip_y, chip_x = seq // side, lax.rem(seq, side)

    def chip_at(dx, dy):
        return lax.rem(chip_y + dy, side) * side + lax.rem(chip_x + dx, side)

    def weight_copies(s, slot):
        return [pltpu.make_async_copy(w.at[s], buf.at[slot, t], w_sem.at[slot, 2 * o + t])
                for o, (buf, pair) in enumerate(((win, (wc, wp)), (wout, (wr, ws)))) for t, w in enumerate(pair)]

    x_in = pltpu.make_async_copy(x_ref, xv, self_sem)
    x_in.start()
    for c in weight_copies(0, 0):
        c.start()
    halo_in[0] = jnp.zeros(halo_in.shape[1:], F32)
    skip[...] = jnp.zeros_like(skip)

    barrier = pltpu.get_barrier_semaphore()

    def greet(k, _):
        pl.semaphore_signal(barrier, inc=1, device_id={"sp": lax.rem(me + k, n)}, device_id_type=pl.DeviceIdType.MESH)
        return 0
    lax.fori_loop(1, n, greet, 0)
    x_in.wait()
    pl.semaphore_wait(barrier, n - 1)

    slot_x = pl.ds(lax.rem(me, srcs) * seq_dev, seq_dev)

    def x_copy(b):
        return pltpu.make_async_remote_copy(
            src_ref=xv.at[b], dst_ref=xbuf.at[slot_x], send_sem=x_send, recv_sem=x_recv,
            device_id={"sp": b * parts + my_part}, device_id_type=pl.DeviceIdType.MESH)

    def x_start(b):
        @pl.when(b * parts + my_part != me)
        def _():
            x_copy(b).start()

        @pl.when(b * parts + my_part == me)
        def _():
            pltpu.make_async_copy(x_ref.at[b], xbuf.at[slot_x], x_recv).start()
    for dx, dy, _ in send_order(side, 1):
        x_start(chip_at(dx, dy))

    pltpu.make_async_copy(xbuf, xbuf, x_recv).wait()
    store_rows(h.at[0], reach, xbuf[...].astype(F32))

    def layer(s, i, slot):
        src, dst = h.at[i % 2], h.at[(i + 1) % 2]
        d = 2 ** i
        for g in range(h.shape[1]):
            src[g, pl.ds(reach - d, d), :] = halo_in[s * part, g, pl.ds(d, d), :]
            halo_out[s, g, pl.ds(d, d), :] = src[g, pl.ds(reach + rows - d, d), :]
        cur = load_rows(src, reach, rows)
        past = load_rows(src, reach - d, rows).astype(BF16)
        z = (jnp.dot(cur.astype(BF16), win[slot, 0, i], preferred_element_type=F32)
             + jnp.dot(past, win[slot, 1, i], preferred_element_type=F32))
        a = gated(z)
        store_rows(dst, reach, cur + jnp.dot(a, wout[slot, 0, i], preferred_element_type=F32))
        store_rows(skip, 0, load_rows(skip, 0, rows) + jnp.dot(a, wout[slot, 1, i], preferred_element_type=F32))

    def halo_copy(s):
        return pltpu.make_async_remote_copy(
            src_ref=halo_out.at[s], dst_ref=halo_in.at[s], send_sem=halo_send, recv_sem=halo_recv.at[s],
            device_id={"sp": jnp.minimum(me + 1, n - 1)}, device_id_type=pl.DeviceIdType.MESH)

    def stack(s, slot):
        for c in weight_copies(s, slot):
            c.wait()

        @pl.when(s + 1 < stacks)
        def _():
            for c in weight_copies(s + 1, 1 - slot):
                c.start()

        @pl.when(part > 0)
        def _():
            halo_copy(s).wait_recv()
        for i in range(cycle):
            layer(s, i, slot)

        @pl.when(part < parts - 1)
        def _():
            halo_copy(s).start()

    def stack_group(q, _):
        for r in range(unroll):
            s = q * unroll + r
            stack(s, r % 2 if unroll % 2 == 0 else lax.rem(s, 2))
        return 0
    lax.fori_loop(0, stacks // unroll, stack_group, 0)

    per = rows // n
    for j in range(n):
        for g in range(h.shape[1]):
            stage[j, 0, :, g * LANES:(g + 1) * LANES] = h[0, g, pl.ds(reach + j, per, stride=n), :]
            stage[j, 1, :, g * LANES:(g + 1) * LANES] = skip[g, pl.ds(j, per, stride=n), :]

    def out_copy(target, source):
        return pltpu.make_async_remote_copy(
            src_ref=stage.at[target], dst_ref=out_ref.at[source // parts, lax.rem(source, parts)],
            send_sem=o_send, recv_sem=o_recv,
            device_id={"sp": target}, device_id_type=pl.DeviceIdType.MESH)

    for dx, dy, dc in send_order(side, parts):
        if (dx, dy, dc) != (0, 0, 0):
            out_copy(chip_at(dx, dy) * parts + lax.rem(part + dc, parts), me).start()
    pltpu.make_async_copy(stage.at[me], out_ref.at[seq, part], o_recv).start()

    blocks = batch - (my_part == part).astype(jnp.int32)
    for count in (batch - 1, batch):
        @pl.when(blocks == count)
        def _():
            pltpu.make_async_copy(xv.at[pl.ds(0, count)], xv.at[pl.ds(0, count)], x_send).wait()

    @pl.when(part < parts - 1)
    def _():
        pltpu.make_async_copy(halo_out, halo_out, halo_send).wait()
    pltpu.make_async_copy(stage.at[pl.ds(0, n - 1)], stage.at[pl.ds(0, n - 1)], o_send).wait()
    pltpu.make_async_copy(out_ref, out_ref, o_recv).wait()


def split_kernel(both_ref, h_ref, skip_ref, sem):
    copies = [pltpu.make_async_copy(both_ref.at[:, :, t], ref, sem.at[t]) for t, ref in enumerate((h_ref, skip_ref))]
    for c in copies:
        c.start()
    for c in copies:
        c.wait()


def solution(mesh):
    n = mesh.shape["sp"]

    def local_stack(x_loc, w_cur, w_past, w_res, w_skip):
        batch, seq_dev, channels = x_loc.shape
        stacks, cycle = w_cur.shape[:2]
        parts = n // batch
        srcs = n // parts
        rows, halves, reach = seq_dev * srcs, channels // LANES, 2 ** (cycle - 1)
        per = rows // n
        any_space = pl.BlockSpec(memory_space=pl.ANY)
        dma = pltpu.SemaphoreType.DMA
        out = pl.pallas_call(
            functools.partial(stack_kernel, n, UNROLL),
            out_shape=jax.ShapeDtypeStruct((batch, parts, 2, per, channels), F32),
            in_specs=[pl.BlockSpec(memory_space=pltpu.HBM)] * 5,
            out_specs=any_space,
            scratch_shapes=[
                pltpu.VMEM(x_loc.shape, BF16),
                pltpu.VMEM((rows, channels), BF16),
                pltpu.VMEM((2, halves, reach + rows, LANES), F32),
                pltpu.VMEM((halves, rows, LANES), F32),
                pltpu.VMEM((2, 2) + w_cur.shape[1:], BF16),
                pltpu.VMEM((2, 2) + w_res.shape[1:], BF16),
                pltpu.VMEM((stacks, halves, 2 * reach, LANES), F32),
                pltpu.VMEM((stacks, halves, 2 * reach, LANES), F32),
                pltpu.VMEM((n, 2, per, channels), F32),
                dma((2, 4)), dma, dma, dma, dma((stacks,)), dma, dma, dma,
            ],
            compiler_params=pltpu.CompilerParams(collective_id=0, has_side_effects=True, vmem_limit_bytes=VMEM << 20),
            name="conv_stack",
        )(pltpu.with_memory_space_constraint(x_loc, pltpu.HBM), w_cur, w_past, w_res, w_skip)
        shape = (batch, 1, parts * per, channels)
        one = jax.ShapeDtypeStruct((batch, parts, per, channels), F32)
        h_out, skip_out = pl.pallas_call(
            split_kernel,
            out_shape=[one, one],
            in_specs=[any_space], out_specs=[any_space] * 2,
            scratch_shapes=[dma((2,))],
            compiler_params=pltpu.CompilerParams(vmem_limit_bytes=VMEM << 20),
            name="split",
        )(out)
        return h_out.reshape(shape), skip_out.reshape(shape)

    return jax.shard_map(local_stack, mesh=mesh, in_specs=(P("dp", "sp", None), P(), P(), P(), P()), out_specs=(P("dp", "sp", None, None), P("dp", "sp", None, None)), check_vma=False)
```

time: 93.3 us -> 90 us (0.965)
  local copies, waits for them, and re-layouts: 2.29 us -> 0 us
    slice x1 -> x0, local copies, waits for them, and re-layouts: 2.29 us -> none  [local_stack(): return (out[:, :, 0].reshape(shape), out[:, :, 1].reshape(shape))]
    pallas_call x1 -> x2, Pallas kernels: 90.2 us -> 89.3 us  [the longest x1 88.3 us: local_stack(): pl.pallas_call(functools.partial(stack_kernel, n, UNROLL), out_shape=jax....]
where the time goes in v2:
time: 90 us
  Pallas kernels  89.3 us (99%)
    pallas_call x1, Pallas kernels, local_stack(): pl.pallas_call(functools.partial(stack_kernel, n, UNROLL), out_shape=jax....  88.3 us

profile of v2, /device:TPU:97, one launch (start us, length us, event | category | flops | bytes accessed | tf_op | source)
XLA Modules:
  0.0 90.0 jit_solution(9938902719261476032)
XLA Ops:
  0.6 88.3 %conv_stack.1.both_ref = f32[16,2,2,16,256]{4,3,2,1,0:T(8,128)S(1)} custom-call(bf16[16,32,256]{2,1,0:T(8,128)(2,1)} %x_ref.1, bf16[16,8,256,512]{3,2,1,0:T(8,128)(2,1)} %wc.1, bf16[16,8,256,512]{3,2,1,0:T(8,128)(2,1)} %wp.1, bf16[16,8,256,256]{3,2,1,0:T(8,128)(2,1)} %wr.1, bf16[16,8,256,256]{3,2,1,0:T(8,128)(2,1)} %ws.1), custom_call_target="tpu_custom_call" | custom-call | tf_op jit(solution)/shard_map/conv_stack/pallas_call | solution.py:191
  89.0 1.0 %split.1 = (f32[16,2,16,256]{3,2,1,0:T(8,128)}, f32[16,2,16,256]{3,2,1,0:T(8,128)}) custom-call(f32[16,2,2,16,256]{4,3,2,1,0:T(8,128)S(1)} %conv_stack.1.both_ref), custom_call_target="tpu_custom_call" | custom-call | tf_op jit(solution)/shard_map/split/pallas_call | solution.py:213

commit v3 on v2

--- a/solution.py
+++ b/solution.py
@@ -10,6 +10,7 @@
 
 F32, BF16 = jnp.float32, jnp.bfloat16
 LANES = 128
+SUBLANES = 8
 UNROLL = 2
 VMEM = 50
 
@@ -100,7 +101,11 @@
             src[g, pl.ds(reach - d, d), :] = halo_in[s * part, g, pl.ds(d, d), :]
             halo_out[s, g, pl.ds(d, d), :] = src[g, pl.ds(reach + rows - d, d), :]
         cur = load_rows(src, reach, rows)
-        past = load_rows(src, reach - d, rows).astype(BF16)
+        if d < SUBLANES:
+            past = pltpu.roll(jnp.concatenate([load_rows(src, reach - SUBLANES, SUBLANES), cur], axis=0), d, 0)[SUBLANES:]
+        else:
+            past = load_rows(src, reach - d, rows)
+        past = past.astype(BF16)
         z = (jnp.dot(cur.astype(BF16), win[slot, 0, i], preferred_element_type=F32)
              + jnp.dot(past, win[slot, 1, i], preferred_element_type=F32))
         a = gated(z)

time: 90 us -> 88.6 us (0.984)
  Pallas kernels: 89.3 us -> 87.9 us
    pallas_call x1, Pallas kernels: 88.3 us -> 86.9 us  [local_stack(): pl.pallas_call(functools.partial(stack_kernel, n, UNROLL), out_shape=jax....]
where the time goes in v3:
time: 88.6 us; the launch traced here: 88.5 us
  Pallas kernels  87.9 us (99%)
    pallas_call x1, Pallas kernels, local_stack(): pl.pallas_call(functools.partial(stack_kernel, n, UNROLL), out_shape=jax....  86.9 us

profile of v3, /device:TPU:97, one launch (start us, length us, event | category | flops | bytes accessed | tf_op | source)
XLA Modules:
  0.0 88.5 jit_solution(15498978656182048984)
XLA Ops:
  0.6 86.9 %conv_stack.1.both_ref = f32[16,2,2,16,256]{4,3,2,1,0:T(8,128)S(1)} custom-call(bf16[16,32,256]{2,1,0:T(8,128)(2,1)} %x_ref.1, bf16[16,8,256,512]{3,2,1,0:T(8,128)(2,1)} %wc.1, bf16[16,8,256,512]{3,2,1,0:T(8,128)(2,1)} %wp.1, bf16[16,8,256,256]{3,2,1,0:T(8,128)(2,1)} %wr.1, bf16[16,8,256,256]{3,2,1,0:T(8,128)(2,1)} %ws.1), custom_call_target="tpu_custom_call" | custom-call | tf_op jit(solution)/shard_map/conv_stack/pallas_call | solution.py:196
  87.5 1.0 %split.1 = (f32[16,2,16,256]{3,2,1,0:T(8,128)}, f32[16,2,16,256]{3,2,1,0:T(8,128)}) custom-call(f32[16,2,2,16,256]{4,3,2,1,0:T(8,128)S(1)} %conv_stack.1.both_ref), custom_call_target="tpu_custom_call" | custom-call | tf_op jit(solution)/shard_map/split/pallas_call | solution.py:218

commit v4 on v3

--- a/solution.py
+++ b/solution.py
@@ -80,17 +80,17 @@
             src_ref=xv.at[b], dst_ref=xbuf.at[slot_x], send_sem=x_send, recv_sem=x_recv,
             device_id={"sp": b * parts + my_part}, device_id_type=pl.DeviceIdType.MESH)
 
-    def x_start(b):
-        @pl.when(b * parts + my_part != me)
-        def _():
-            x_copy(b).start()
-
-        @pl.when(b * parts + my_part == me)
-        def _():
-            pltpu.make_async_copy(x_ref.at[b], xbuf.at[slot_x], x_recv).start()
     for dx, dy, _ in send_order(side, 1):
-        x_start(chip_at(dx, dy))
-
+        if (dx, dy) != (0, 0):
+            x_copy(chip_at(dx, dy)).start()
+
+    @pl.when(my_part != part)
+    def _():
+        x_copy(seq).start()
+
+    @pl.when(my_part == part)
+    def _():
+        pltpu.make_async_copy(x_ref.at[seq], xbuf.at[slot_x], x_recv).start()
     pltpu.make_async_copy(xbuf, xbuf, x_recv).wait()
     store_rows(h.at[0], reach, xbuf[...].astype(F32))
 
@@ -144,10 +144,10 @@
     lax.fori_loop(0, stacks // unroll, stack_group, 0)
 
     per = rows // n
-    for j in range(n):
+    for t, (state, first) in enumerate(((h.at[0], reach), (skip, 0))):
         for g in range(h.shape[1]):
-            stage[j, 0, :, g * LANES:(g + 1) * LANES] = h[0, g, pl.ds(reach + j, per, stride=n), :]
-            stage[j, 1, :, g * LANES:(g + 1) * LANES] = skip[g, pl.ds(j, per, stride=n), :]
+            by_turn = state[g, pl.ds(first, rows), :].reshape(per, n, LANES)
+            stage[:, t, :, g * LANES:(g + 1) * LANES] = jnp.swapaxes(by_turn, 0, 1)
 
     def out_copy(target, source):
         return pltpu.make_async_remote_copy(

time: 88.6 us -> 88.2 us (level)
  no operation moved by 1% of the time
where the time goes in v4:
time: 88.2 us; the launch traced here: 88.1 us
  Pallas kernels  87.5 us (99%)
    pallas_call x1, Pallas kernels, local_stack(): pl.pallas_call(functools.partial(stack_kernel, n, UNROLL), out_shape=jax....  86.5 us

profile of v4, /device:TPU:97, one launch (start us, length us, event | category | flops | bytes accessed | tf_op | source)
XLA Modules:
  0.0 88.1 jit_solution(833844550314223567)
XLA Ops:
  0.6 86.5 %conv_stack.1.both_ref = f32[16,2,2,16,256]{4,3,2,1,0:T(8,128)S(1)} custom-call(bf16[16,32,256]{2,1,0:T(8,128)(2,1)} %x_ref.1, bf16[16,8,256,512]{3,2,1,0:T(8,128)(2,1)} %wc.1, bf16[16,8,256,512]{3,2,1,0:T(8,128)(2,1)} %wp.1, bf16[16,8,256,256]{3,2,1,0:T(8,128)(2,1)} %wr.1, bf16[16,8,256,256]{3,2,1,0:T(8,128)(2,1)} %ws.1), custom_call_target="tpu_custom_call" | custom-call | tf_op jit(solution)/shard_map/conv_stack/pallas_call | solution.py:196
  87.1 1.0 %split.1 = (f32[16,2,16,256]{3,2,1,0:T(8,128)}, f32[16,2,16,256]{3,2,1,0:T(8,128)}) custom-call(f32[16,2,2,16,256]{4,3,2,1,0:T(8,128)S(1)} %conv_stack.1.both_ref), custom_call_target="tpu_custom_call" | custom-call | tf_op jit(solution)/shard_map/split/pallas_call | solution.py:218

commit v5 on v4

--- a/solution.py
+++ b/solution.py
@@ -54,7 +54,7 @@
         return lax.rem(chip_y + dy, side) * side + lax.rem(chip_x + dx, side)
 
     def weight_copies(s, slot):
-        return [pltpu.make_async_copy(w.at[s], buf.at[slot, t], w_sem.at[slot, 2 * o + t])
+        return [pltpu.make_async_copy(w.at[s], buf.at[slot, t], w_sem.at[slot, o])
                 for o, (buf, pair) in enumerate(((win, (wc, wp)), (wout, (wr, ws)))) for t, w in enumerate(pair)]
 
     x_in = pltpu.make_async_copy(x_ref, xv, self_sem)
@@ -118,8 +118,8 @@
             device_id={"sp": jnp.minimum(me + 1, n - 1)}, device_id_type=pl.DeviceIdType.MESH)
 
     def stack(s, slot):
-        for c in weight_copies(s, slot):
-            c.wait()
+        for o, buf in enumerate((win, wout)):
+            pltpu.make_async_copy(buf.at[slot], buf.at[slot], w_sem.at[slot, o]).wait()
 
         @pl.when(s + 1 < stacks)
         def _():
@@ -208,7 +208,7 @@
                 pltpu.VMEM((stacks, halves, 2 * reach, LANES), F32),
                 pltpu.VMEM((stacks, halves, 2 * reach, LANES), F32),
                 pltpu.VMEM((n, 2, per, channels), F32),
-                dma((2, 4)), dma, dma, dma, dma((stacks,)), dma, dma, dma,
+                dma((2, 2)), dma, dma, dma, dma((stacks,)), dma, dma, dma,
             ],
             compiler_params=pltpu.CompilerParams(collective_id=0, has_side_effects=True, vmem_limit_bytes=VMEM << 20),
             name="conv_stack",

time: 88.2 us -> 88.6 us (level)
  no operation moved by 1% of the time
where the time goes in v5:
time: 88.6 us; the launch traced here: 88.5 us
  Pallas kernels  87.9 us (99%)
    pallas_call x1, Pallas kernels, local_stack(): pl.pallas_call(functools.partial(stack_kernel, n, UNROLL), out_shape=jax....  86.9 us

profile of v5, /device:TPU:97, one launch (start us, length us, event | category | flops | bytes accessed | tf_op | source)
XLA Modules:
  0.0 88.5 jit_solution(8765094474739248741)
XLA Ops:
  0.6 86.9 %conv_stack.1.both_ref = f32[16,2,2,16,256]{4,3,2,1,0:T(8,128)S(1)} custom-call(bf16[16,32,256]{2,1,0:T(8,128)(2,1)} %x_ref.1, bf16[16,8,256,512]{3,2,1,0:T(8,128)(2,1)} %wc.1, bf16[16,8,256,512]{3,2,1,0:T(8,128)(2,1)} %wp.1, bf16[16,8,256,256]{3,2,1,0:T(8,128)(2,1)} %wr.1, bf16[16,8,256,256]{3,2,1,0:T(8,128)(2,1)} %ws.1), custom_call_target="tpu_custom_call" | custom-call | tf_op jit(solution)/shard_map/conv_stack/pallas_call | solution.py:196
  87.5 1.0 %split.1 = (f32[16,2,16,256]{3,2,1,0:T(8,128)}, f32[16,2,16,256]{3,2,1,0:T(8,128)}) custom-call(f32[16,2,2,16,256]{4,3,2,1,0:T(8,128)S(1)} %conv_stack.1.both_ref), custom_call_target="tpu_custom_call" | custom-call | tf_op jit(solution)/shard_map/split/pallas_call | solution.py:218
